TPU v7x, 32 devices: a whole 2x2x4 slice. The times are simulated.
32 devices in a mesh: samp: 8 (over z, x), feat: 4 (over y, core).
Axes of the slice: x: 2, y: 2, z: 4, core: 2. Of those that a mesh axis runs over, the one named last changes fastest.
Arguments:
- inputs: bfloat16 [16384, 96], P('samp'), may hold values from -6 to 6
- frequencies: bfloat16 [96, 16384], P(None, 'feat'), may hold values from -0.625 to 0.625
- phases: float32 [16384], P('feat'), may hold values from -3.140625 to 3.140625
- targets: float32 [16384], P('samp'), may hold values from -12 to 12
- block_order: int32 [16384], P('samp'), may hold values from 0 to 2047, as said below
Outputs:
- weights: float32 [16384], P('feat')
- duals: float32 [16384], P('samp')
- objectives: float32 [4, 2], replicated
Inputs may be any that keep to these rules, and one draw needn't show every extreme that they name: `block_order`: within each aligned run of 2048 samples, a permutation of 0 to 2047.
All inputs are finite; a program needn't handle non-finite values.
Results may differ from a plain program's by a relative error of at most 0.0054.
The roundings to bfloat16 on the way count: a program that leaves them out, or rounds other values in their place, can miss the bound.
Values may be sent and summed in bfloat16 or wider, within the bound.
A program may use at most 64 MiB of HBM per device.

v0:
```python
import math

import jax
import jax.numpy as jnp
from jax import lax
from jax.sharding import PartitionSpec as P

FEATURES = 16384
BLOCK = 256
ROUNDS = 4


def solve_block(factor, vector):
    return jax.scipy.linalg.cho_solve((factor, True), vector)


def on_device(inputs, frequencies, phases, targets, block_order):
    row_count = inputs.shape[0]
    groups = lax.axis_size("samp")
    sample_total = row_count * groups
    ridge = 1.0 / BLOCK
    step_scale = BLOCK / sample_total
    block_count = row_count // BLOCK
    feat_count = lax.axis_size("feat")
    own_blocks = block_count // feat_count
    picked = inputs[block_order]
    wanted = targets[block_order]
    angles = jnp.dot(picked, frequencies, preferred_element_type=jnp.float32)
    features = (math.sqrt(2.0 / FEATURES) * jnp.cos(angles + phases)).astype(jnp.bfloat16)
    blocked = features.reshape(block_count, BLOCK, features.shape[1])
    gram_sums = jnp.einsum("bid,bjd->bij", blocked, blocked, preferred_element_type=jnp.float32)
    gram_sums = lax.psum_scatter(gram_sums, "feat", scatter_dimension=0, tiled=True)
    factors = jnp.linalg.cholesky(gram_sums + jnp.eye(BLOCK, dtype=jnp.float32))
    duals = jnp.zeros((row_count,), jnp.float32)
    margins = jnp.zeros((row_count,), jnp.float32)
    weights = jnp.zeros((features.shape[1],), jnp.float32)
    collected = []
    for round_index in range(ROUNDS):
        residual = (wanted - duals - margins).reshape(block_count, BLOCK)
        first = lax.axis_index("feat") * own_blocks
        own_residual = lax.dynamic_slice_in_dim(residual, first, own_blocks, 0)
        own_update = jax.vmap(solve_block)(factors, own_residual)
        update = lax.all_gather(own_update, "feat", axis=0, tiled=True).reshape(row_count)
        duals = duals + update
        update_bf = update.astype(jnp.bfloat16)
        step_term = jnp.dot(update_bf, features, preferred_element_type=jnp.float32) * step_scale
        weights = weights + lax.psum(step_term, "samp")
        weight_bf = weights.astype(jnp.bfloat16)
        norm_part = jnp.sum(weights * weights)
        partial_value = jnp.dot(features, weight_bf, preferred_element_type=jnp.float32)
        margins, norm_feat = lax.psum((partial_value, norm_part), "feat")
        squares = jnp.sum((margins - wanted) ** 2)
        dual_sum = jnp.sum(duals * wanted - 0.5 * duals * duals)
        local_stats = jnp.stack([squares, dual_sum, norm_feat / groups])
        collected.append(lax.psum(local_stats, "samp"))
    totals = jnp.stack(collected)
    primal_value = totals[:, 0] / (2.0 * sample_total) + 0.5 * ridge * totals[:, 2]
    dual_value = totals[:, 1] / sample_total - 0.5 * ridge * totals[:, 2]
    objectives = jnp.stack([primal_value, dual_value], axis=1)
    restored = jnp.zeros_like(duals).at[block_order].set(duals)
    return (weights, restored, objectives)


def solution(mesh):
    placed = (P("samp", None), P(None, "feat"), P("feat"), P("samp"), P("samp"))
    return jax.shard_map(
        on_device,
        mesh=mesh,
        in_specs=placed,
        out_specs=(P("feat"), P("samp"), P()),
        check_vma=False,
    )
```

profile of v0, /device:TPU:0, one launch (start us, length us, event | category | flops | bytes accessed | tf_op | source)
XLA Modules:
  0.0 609.5 jit_solution(5051314664634490128)
XLA Ops:
  9.3 6.2 %gather_fusion = bf16[2048,96]{1,0:T(8,128)(2,1)S(1)} fusion(bf16[2048,96]{1,0:T(8,128)(2,1)S(1)} %copy.38, s32[2048]{0:T(1024)S(1)} %get-tuple-element.88), kind=kCustom, calls=%fused_computation | custom fusion | bytes 794624 | tf_op jit(solution)/shard_map/gather | solution.py:26
  15.5 120.3 %multiply_convert_fusion = bf16[2048,4096]{1,0:T(8,128)(2,1)} fusion(f32[4096]{0:T(1024)} %param.9, bf16[2048,96]{1,0:T(8,128)(2,1)S(1)} %gather_fusion, bf16[96,4096]{1,0:T(8,128)(2,1)S(1)} %copy-done), kind=kOutput, calls=%fused_computation.5 | convolution fusion | flops 1635778560 | bytes 17973248 | tf_op jit(solution)/shard_map/dot_general | solution.py:28
  135.8 14.3 %fusion.53 = f32[8,256,256]{1,2,0:T(8,128)} fusion(bf16[8,256,4096]{2,1,0:T(8,128)(2,1)} %bitcast.299), kind=kOutput, calls=%fused_computation.123 | convolution fusion | flops 4294967296 | bytes 18874368 | tf_op jit(solution)/shard_map/bid,bjd->bij/dot_general | solution.py:31
  150.1 11.8 %gather_fusion.1 = f32[2048]{0:T(1024)S(1)} fusion(f32[2048]{0:T(1024)S(1)} %copy-done.1, s32[2048]{0:T(1024)S(1)} %get-tuple-element.88), kind=kCustom, calls=%fused_computation.1 | custom fusion | bytes 24576 | tf_op jit(solution)/shard_map/gather | solution.py:27
  162.0 22.1 %reduce-scatter.2.cloned.1.call-done = f32[2,256,256]{1,2,0:T(8,128)} async-done(((f32[8,256,256]{1,2,0:T(8,128)}), f32[2,256,256]{1,2,0:T(8,128)}) %reduce-scatter.2.cloned.1.call-update) | async-done | bytes 524304 | tf_op jit(solution)/shard_map/reduce_scatter | solution.py:32
  186.6 23.5 %custom-call.18 = f32[2,128,128]{2,1,0:T(8,128)S(1)} custom-call(f32[2,128,128]{2,1,0:T(8,128)S(1)} %cholesky.122), custom_call_target="Cholesky" | custom-call | tf_op jit(solution)/shard_map/jit(cholesky)/cholesky | solution.py:33
  210.1 19.7 %custom-call.19 = f32[2,1,128,128]{2,3,1,0:T(8,128)S(1)} custom-call(f32[2,1,128,128]{3,2,1,0:T(8,128)S(1)} %select_bitcast_fusion), custom_call_target="InvertDiagBlocksLowerTriangular" | custom-call | tf_op jit(solution)/shard_map/jit(cholesky)/cholesky | solution.py:33
  230.5 23.9 %custom-call.20 = f32[2,128,128]{2,1,0:T(8,128)S(1)} custom-call(f32[2,128,128]{2,1,0:T(8,128)S(1)} %convolution_subtract_fusion), custom_call_target="Cholesky" | custom-call | tf_op jit(solution)/shard_map/jit(cholesky)/cholesky | solution.py:33
  258.8 39.3 %custom-call.24 = f32[2,2,128,128]{2,3,1,0:T(8,128)S(1)} custom-call(f32[2,2,128,128]{3,2,1,0:T(8,128)S(1)} %bitcast.353), custom_call_target="InvertDiagBlocksLowerTriangular" | custom-call | tf_op jit(solution)/shard_map/vmap(jit(_cho_solve))/triangular_solve | solution.py:14
  305.1 8.0 %fusion.54 = f32[1,4096]{1,0:T(1,128)S(1)} fusion(bf16[2048,1]{0,1:T(2,128)(2,1)S(1)} %reshape.196, bf16[2048,4096]{1,0:T(8,128)(2,1)} %multiply_convert_fusion), kind=kOutput, calls=%fused_computation.124 | convolution fusion | flops 16777216 | bytes 16797696 | tf_op jit(solution)/shard_map/dot_general | solution.py:46
  313.1 37.3 %psum.112 = f32[4096]{0:T(1024)S(1)} all-reduce(f32[4096]{0:T(1024)S(1)} %broadcast_multiply_fusion.3), channel_id=1, replica_groups=mesh['samp'=8,'feat'=4] {'samp'}, use_global_device_ids=true, to_apply=%region_5.7 | all-reduce | flops 4096 | bytes 32768 | tf_op jit(solution)/shard_map/psum | solution.py:47
  350.5 10.2 %fusion.55 = f32[1,2048]{1,0:T(1,128)S(1)} fusion(bf16[2048,4096]{1,0:T(8,128)(2,1)} %multiply_convert_fusion, bf16[4096,1]{0,1:T(2,128)(2,1)S(1)} %reshape.198), kind=kOutput, calls=%fused_computation.125 | convolution fusion | flops 16777216 | bytes 16793600 | tf_op jit(solution)/shard_map/dot_general | solution.py:50
  373.7 8.0 %fusion.56 = f32[1,4096]{1,0:T(1,128)S(1)} fusion(bf16[2048,1]{0,1:T(2,128)(2,1)S(1)} %reshape.211, bf16[2048,4096]{1,0:T(8,128)(2,1)} %multiply_convert_fusion), kind=kOutput, calls=%fused_computation.126 | convolution fusion | flops 16777216 | bytes 16797696 | tf_op jit(solution)/shard_map/dot_general | solution.py:46
  381.8 33.0 %psum.114 = f32[4096]{0:T(1024)S(1)} all-reduce(f32[4096]{0:T(1024)S(1)} %broadcast_multiply_fusion.2), channel_id=1, replica_groups=mesh['samp'=8,'feat'=4] {'samp'}, use_global_device_ids=true, to_apply=%region_7.9 | all-reduce | flops 4096 | bytes 32768 | tf_op jit(solution)/shard_map/psum | solution.py:47
  415.4 10.2 %fusion.57 = f32[1,2048]{1,0:T(1,128)S(1)} fusion(bf16[2048,4096]{1,0:T(8,128)(2,1)} %multiply_convert_fusion, bf16[4096,1]{0,1:T(2,128)(2,1)S(1)} %reshape.213), kind=kOutput, calls=%fused_computation.127 | convolution fusion | flops 16777216 | bytes 16793600 | tf_op jit(solution)/shard_map/dot_general | solution.py:50
  438.6 8.0 %fusion.58 = f32[1,4096]{1,0:T(1,128)S(1)} fusion(bf16[2048,1]{0,1:T(2,128)(2,1)S(1)} %reshape.226, bf16[2048,4096]{1,0:T(8,128)(2,1)} %multiply_convert_fusion), kind=kOutput, calls=%fused_computation.128 | convolution fusion | flops 16777216 | bytes 16797696 | tf_op jit(solution)/shard_map/dot_general | solution.py:46
  446.7 33.0 %psum.116 = f32[4096]{0:T(1024)S(1)} all-reduce(f32[4096]{0:T(1024)S(1)} %broadcast_multiply_fusion.1), channel_id=1, replica_groups=mesh['samp'=8,'feat'=4] {'samp'}, use_global_device_ids=true, to_apply=%region_9.11 | all-reduce | flops 4096 | bytes 32768 | tf_op jit(solution)/shard_map/psum | solution.py:47
  480.3 10.2 %fusion.59 = f32[1,2048]{1,0:T(1,128)S(1)} fusion(bf16[2048,4096]{1,0:T(8,128)(2,1)} %multiply_convert_fusion, bf16[4096,1]{0,1:T(2,128)(2,1)S(1)} %reshape.228), kind=kOutput, calls=%fused_computation.129 | convolution fusion | flops 16777216 | bytes 16793600 | tf_op jit(solution)/shard_map/dot_general | solution.py:50
  503.3 8.0 %fusion.60 = f32[1,4096]{1,0:T(1,128)S(1)} fusion(bf16[2048,1]{0,1:T(2,128)(2,1)S(1)} %reshape.241, bf16[2048,4096]{1,0:T(8,128)(2,1)} %multiply_convert_fusion), kind=kOutput, calls=%fused_computation.130 | convolution fusion | flops 16777216 | bytes 16797696 | tf_op jit(solution)/shard_map/dot_general | solution.py:46
  511.3 33.2 %psum.118 = f32[4096]{0:T(1024)S(1)} all-reduce(f32[4096]{0:T(1024)S(1)} %broadcast_multiply_fusion), channel_id=1, replica_groups=mesh['samp'=8,'feat'=4] {'samp'}, use_global_device_ids=true, to_apply=%region_11.13 | all-reduce | flops 4096 | bytes 32768 | tf_op jit(solution)/shard_map/psum | solution.py:47
  544.6 10.2 %fusion.61 = f32[1,2048]{1,0:T(1,128)S(1)} fusion(bf16[2048,4096]{1,0:T(8,128)(2,1)} %multiply_convert_fusion, bf16[4096,1]{0,1:T(2,128)(2,1)S(1)} %reshape.243), kind=kOutput, calls=%fused_computation.131 | convolution fusion | flops 16777216 | bytes 16793600 | tf_op jit(solution)/shard_map/dot_general | solution.py:50
  555.4 11.2 %all-reduce.2 = (f32[]{:T(128)}, f32[2048]{0:T(1024)S(1)}, f32[]{:T(128)}, f32[]{:T(128)}, f32[]{:T(128)}) all-reduce(f32[]{:T(128)} %multiply_reduce_fusion, f32[2048]{0:T(1024)S(1)} %bitcast.317, f32[]{:T(128)} %get-tuple-element.75, f32[]{:T(128)} %get-tuple-element.73, ...), channel_id=1, replica_groups=mesh['samp'=8,'feat'=4] {'feat'}, use_global_device_ids=true, to_apply=%region_32.34 | all-reduce | flops 2052 | bytes 16416 | tf_op jit(solution)/shard_map/psum | solution.py:51
  575.7 17.1 %all-reduce.1 = (f32[1,3]{1,0:T(1,128)S(1)}, f32[1,3]{1,0:T(1,128)S(1)}, f32[1,3]{1,0:T(1,128)S(1)}, f32[1,3]{1,0:T(1,128)S(1)}) all-reduce(f32[1,3]{1,0:T(1,128)S(1)} %maximum_bitcast_fusion.7, f32[1,3]{1,0:T(1,128)S(1)} %maximum_bitcast_fusion.6, ...), channel_id=1, replica_groups=mesh['samp'=8,'feat'=4] {'samp'}, use_global_device_ids=true, to_apply=%region_33.35 | all-reduce | flops 12 | bytes 96 | tf_op jit(solution)/shard_map/psum | solution.py:55
  593.6 8.6 %scatter_custom_fusion = f32[2048]{0:T(1024)} fusion(s32[2048]{0:T(1024)S(1)} %get-tuple-element.87, f32[2048]{0:T(1024)S(1)} %add.131, f32[]{:T(128)} %constant.114.clone.1), kind=kCustom, calls=%fused_computation.85 | custom fusion | bytes 8196 | tf_op jit(solution)/shard_map/scatter | solution.py:60
  (136 shorter events, 68.8 us)
Async XLA Ops:
  7.2 8.3 %copy-start = (bf16[96,4096]{1,0:T(8,128)(2,1)S(1)}, bf16[96,4096]{1,0:T(8,128)(2,1)}, u32[]{:S(2)}) copy-start(bf16[96,4096]{1,0:T(8,128)(2,1)} %param.8) | copy-start | bytes 2359300
  7.2 177.0 %reduce-scatter.2.cloned.1.call-start = ((), (), s32[]{:S(2)}) async-start(), calls=%async_computation.1 | async-start | bytes 2621440 | tf_op jit(solution)/shard_map/reduce_scatter | solution.py:32
  135.8 14.3 %copy-start.1 = (f32[2048]{0:T(1024)S(1)}, f32[2048]{0:T(1024)}, u32[]{:S(2)}) copy-start(f32[2048]{0:T(1024)} %param.10) | copy-start | bytes 24580
  544.5 57.7 %copy-start.2 = (f32[4096]{0:T(1024)}, f32[4096]{0:T(1024)S(1)}, u32[]{:S(2)}) copy-start(f32[4096]{0:T(1024)S(1)} %get-tuple-element.78) | copy-start | bytes 49156
Sparse Core Ops, SparseCore 0:
  150.2 33.9 reduce-scatter.1
where the time goes:
time: 619 us; the launch traced here: 610 us
  matrix products  215 us (35%)
  blocking collectives  204 us (33%)
  other arithmetic  119 us (19%)
  local copies, waits for them, and re-layouts  33 us (5%)
  waiting for transfers between devices  22.1 us (4%)
  between operations  17.4 us (3%)
    psum x4, blocking collectives, on_device(): weights = weights + lax.psum(step_term, 'samp')  136 us
    dot_general x1, matrix products, on_device(): angles = jnp.dot(picked, frequencies, preferred_element_type=jnp.float32)  120 us
    another operation x9, other arithmetic, on_device(): factors = jnp.linalg.cholesky(gram_sums + jnp.eye(BLOCK, dtype=jnp.float32))  67.3 us
    dot_general x4, matrix products, on_device(): jnp.dot(features, weight_bf, preferred_element_type=jnp.float32)  40.7 us
    another operation x13, other arithmetic, solve_block(): return jax.scipy.linalg.cho_solve((factor, True), vector)  39.6 us
    dot_general x4, matrix products, on_device(): jnp.dot(update_bf, features, preferred_element_type=jnp.float32)  32.2 us
    psum x4, blocking collectives, on_device(): margins, norm_feat = lax.psum((partial_value, norm_part), 'feat')  29.2 us
    reduce_scatter x1, waiting for transfers between devices, on_device(): lax.psum_scatter(gram_sums, 'feat', scatter_dimension=0, tiled=True)  22.1 us
  transfers between devices with their start and end apart: 1, of which 1 were waited for; matrix products, arithmetic and copies ran while one was open for 2% of the time, Pallas kernels for 0%

commit v1 on v0

v1 whole, which is shorter than its diff:
```python
import functools
import math

import jax
import jax.numpy as jnp
import numpy as np
from jax import lax
from jax.experimental import pallas as pl
from jax.experimental.pallas import tpu as pltpu
from jax.sharding import PartitionSpec as P

FEATURES = 16384
BLOCK = 256
ROUNDS = 4
LANES = 128
CHUNK = 512
MESH = pl.DeviceIdType.MESH
F32 = jnp.float32
BF16 = jnp.bfloat16


def cosine_coefficients():
    nodes = np.cos((np.arange(400) + 0.5) * np.pi / 400)
    square = (nodes + 1.0) / 8.0
    values = math.sqrt(2.0 / FEATURES) * np.cos(2.0 * np.pi * np.sqrt(square))
    fit = np.polynomial.chebyshev.Chebyshev.fit(square, values, 5, domain=[0.0, 0.25])
    return [float(c) for c in fit.convert(kind=np.polynomial.Polynomial).coef]


COEFS = cosine_coefficients()


def nn(a, b, precision=None):
    return lax.dot_general(a, b, (((1,), (0,)), ((), ())), precision=precision, preferred_element_type=F32)


def nt(a, b):
    return lax.dot_general(a, b, (((1,), (1,)), ((), ())), preferred_element_type=F32)


def halves(a):
    high = a.astype(BF16)
    return high, (a - high.astype(F32)).astype(BF16)


def thirds(a):
    high = a.astype(BF16)
    rest = a - high.astype(F32)
    middle = rest.astype(BF16)
    return high, middle, (rest - middle.astype(F32)).astype(BF16)


def mm3(a, b):
    a_high, a_low = halves(a)
    b_high, b_low = halves(b)
    return nn(a_high, b_high) + (nn(a_high, b_low) + nn(a_low, b_high))


def mm6(a, b):
    return nn(a, b, lax.Precision.HIGHEST)


def stacked(row):
    high, middle, low = (piece.astype(F32) for piece in thirds(row))
    at = lax.broadcasted_iota(jnp.int32, (8, row.shape[1]), 0)
    return jnp.where(at == 0, high, jnp.where(at == 1, middle, low)).astype(BF16)


def unstacked(rows):
    return rows[0:1] + rows[1:2] + rows[2:3]


def kernel(n_samp, n_feat, inputs, freqs, phases, targets, order, w_out, duals_out, obj_out,
           phi, onehot, wanted, duals, margins, weights, w_wide, d_col, y, gram, gram_in, inverse,
           d_buf, w_buf, m_send, m_buf, s_feat, s_samp,
           g_ssem, g_rsem, d_ssem, d_rsem, w_ssem, w_rsem, m_ssem, m_rsem, f_ssem, f_rsem, t_ssem, t_rsem):
    samp, feat = lax.axis_index("samp"), lax.axis_index("feat")
    rows, width = phi.shape
    blocks = rows // BLOCK
    own = blocks // n_feat
    sample_total = rows * n_samp
    ridge = 1.0 / BLOCK
    step_scale = BLOCK / sample_total
    first = feat * own

    barrier = pltpu.get_barrier_semaphore()
    for k in range(1, n_feat):
        pl.semaphore_signal(barrier, inc=1, device_id=(samp, (feat + k) % n_feat), device_id_type=MESH)
    for k in range(1, n_samp):
        pl.semaphore_signal(barrier, inc=1, device_id=((samp + k) % n_samp, feat), device_id_type=MESH)
    pl.semaphore_wait(barrier, n_feat + n_samp - 2)

    def to_feat(peer, src, dst, ssem, rsem):
        return pltpu.make_async_remote_copy(src_ref=src, dst_ref=dst, send_sem=ssem, recv_sem=rsem,
                                            device_id=(samp, peer), device_id_type=MESH)

    def to_samp(peer, src, dst, ssem, rsem):
        return pltpu.make_async_remote_copy(src_ref=src, dst_ref=dst, send_sem=ssem, recv_sem=rsem,
                                            device_id=(peer, feat), device_id_type=MESH)

    target_rows = stacked(targets[...])

    half = n_feat // 2
    chip, core = feat // 2, feat % 2

    def owner_of(k):
        return ((chip + 1 + k // 2) % half) * 2 + (core + 1 + k % 2) % 2

    def gram_copy(i):
        peer = owner_of(i // own)
        local = i % own
        return to_feat(peer, gram.at[peer * own + local], gram_in.at[feat, local],
                       g_ssem.at[peer, local], g_rsem.at[feat, local])

    def make_block(i, carry):
        block = owner_of(i // own) * own + i % own
        at = pl.ds(pl.multiple_of(block * BLOCK, BLOCK), BLOCK)
        position = lax.broadcasted_iota(jnp.int32, (BLOCK, rows), 1)
        hot = jnp.where(order[at, :] == position, 1.0, 0.0).astype(BF16)
        onehot[at, :] = hot
        wanted[block] = unstacked(nt(target_rows, hot))
        picked = nn(hot, inputs[...]).astype(BF16)
        total = None
        for c in range(0, width, CHUNK):
            turns = nn(picked, freqs[:, c:c + CHUNK]) + phases[:, c:c + CHUNK]
            turns = turns * (0.5 / math.pi)
            turns = turns - jnp.floor(turns + 0.5)
            square = turns * turns
            value = COEFS[5] * square + COEFS[4]
            for coef in COEFS[3::-1]:
                value = value * square + coef
            part = value.astype(BF16)
            phi[at, c:c + CHUNK] = part
            term = nt(part, part)
            total = term if total is None else total + term

        @pl.when(i < blocks - own)
        def _():
            gram[block] = total
            gram_copy(i).start()

        @pl.when(i >= blocks - own)
        def _():
            gram_in[feat, i % own] = total

        return carry

    lax.fori_loop(0, blocks, make_block, 0)
    for i in range(blocks - own):
        peer = (feat + 1 + i // own) % n_feat
        copy = to_feat(peer, gram.at[peer * own + i % own], gram_in.at[peer, i % own],
                       g_ssem.at[peer, i % own], g_rsem.at[peer, i % own])
        copy.wait_recv()
        copy.wait_send()

    eye = jnp.where(lax.broadcasted_iota(jnp.int32, (BLOCK, BLOCK), 0)
                    == lax.broadcasted_iota(jnp.int32, (BLOCK, BLOCK), 1), 1.0, 0.0).astype(F32)
    lows = []
    for local in range(own):
        matrix = eye
        for k in range(n_feat):
            matrix = matrix + gram_in[k, local]
        gram[local] = matrix
        bound = jnp.max(jnp.sum(jnp.abs(matrix), axis=0, keepdims=True), axis=1, keepdims=True) * 1.0001
        low = 1.0 / bound
        scale = 2.0 / (bound + 1.0)
        inverse[local] = scale * (2.0 * eye - scale * matrix)
        lows.append(4.0 * low / ((1.0 + low) * (1.0 + low)))

    def newton(mm):
        def step(i, lows):
            scaled = [(2.0 / (1.0 + lows[k])) * inverse[k] for k in range(own)]
            products = [mm(gram[k], scaled[k]) for k in range(own)]
            for k in range(own):
                inverse[k] = 2.0 * scaled[k] - mm(scaled[k], products[k])
            return tuple(4.0 * low / ((1.0 + low) * (1.0 + low)) for low in lows)
        return step

    lows = lax.fori_loop(0, 5, newton(mm3), tuple(lows))
    lax.fori_loop(0, 2, newton(mm6), lows)

    duals[...] = jnp.zeros_like(duals)
    margins[...] = jnp.zeros_like(margins)
    weights[...] = jnp.zeros_like(weights)
    lane = lax.broadcasted_iota(jnp.int32, (1, LANES), 1)
    ones = jnp.ones((8, LANES), BF16)
    tiles = width // LANES

    def one_round(r, carry):
        mine = pl.ds(first, own)
        for k in range(own):
            residual = wanted[first + k] - duals[first + k] - margins[k]
            delta = mm6(jnp.broadcast_to(residual, (8, BLOCK)), inverse[k])
            d_buf[r, first + k] = delta[0:1]
        sends = []
        for k in range(1, n_feat):
            peer = (feat + k) % n_feat
            copy = to_feat(peer, d_buf.at[r, mine], d_buf.at[r, mine], d_ssem.at[r, peer], d_rsem.at[r, feat])
            copy.start()
            sends.append(copy)
        for k in range(1, n_feat):
            peer = (feat + k) % n_feat
            theirs = pl.ds(peer * own, own)
            to_feat(peer, d_buf.at[r, theirs], d_buf.at[r, theirs], d_ssem.at[r, peer], d_rsem.at[r, peer]).wait_recv()
        for copy in sends:
            copy.wait_send()

        for b in range(blocks):
            delta = d_buf[r, b]
            duals[b] = duals[b] + delta
            rounded = delta.astype(BF16).astype(F32)
            for h in range(0, BLOCK, LANES):
                tile = jnp.broadcast_to(rounded[:, h:h + LANES], (LANES, LANES))
                d_col[pl.ds(b * BLOCK + h, LANES), :] = tile.T

        def down(g, sums):
            at = pl.ds(pl.multiple_of(g * 16, 16), 16)
            column = d_col[at, :]
            result = []
            for c in range(tiles):
                term = phi[at, c * LANES:(c + 1) * LANES].astype(F32) * column
                result.append(sums[c] + (term[0:8] + term[8:16]))
            return tuple(result)

        sums = lax.fori_loop(0, rows // 16, down, tuple(jnp.zeros((8, LANES), F32) for _ in range(tiles)))
        for c in range(tiles):
            w_buf[r, samp, :, c * LANES:(c + 1) * LANES] = jnp.sum(sums[c], axis=0, keepdims=True) * step_scale
        sends = []
        for k in range(1, n_samp):
            peer = (samp + k) % n_samp
            copy = to_samp(peer, w_buf.at[r, samp], w_buf.at[r, samp], w_ssem.at[r, peer], w_rsem.at[r, samp])
            copy.start()
            sends.append(copy)
        for k in range(1, n_samp):
            peer = (samp + k) % n_samp
            to_samp(peer, w_buf.at[r, peer], w_buf.at[r, peer], w_ssem.at[r, peer], w_rsem.at[r, peer]).wait_recv()
        for copy in sends:
            copy.wait_send()

        change = w_buf[r, 0]
        for k in range(1, n_samp):
            change = change + w_buf[r, k]
        updated = weights[...] + change
        weights[...] = updated
        norm = jnp.sum(updated * updated, axis=1, keepdims=True)
        w_wide[...] = jnp.broadcast_to(updated.astype(BF16).astype(F32), (8, width))

        def across(g, carry):
            at = pl.ds(pl.multiple_of(g * 32, 32), 32)
            total = jnp.zeros((4, 8, LANES), F32)
            for c in range(tiles):
                term = phi[at, c * LANES:(c + 1) * LANES].astype(F32).reshape(4, 8, LANES)
                total = total + term * w_wide[:, c * LANES:(c + 1) * LANES][None]
            y[at, :] = total.reshape(32, LANES)
            return carry

        lax.fori_loop(0, rows // 32, across, 0)
        for b in range(blocks):
            high, middle, low = thirds(y[b * BLOCK:(b + 1) * BLOCK, :])
            m_send[r, b] = (nt(ones, high) + (nt(ones, middle) + nt(ones, low)))[0:1]
        for k in range(own):
            m_buf[r, feat, k] = m_send[r, first + k]
        sends = []
        for k in range(1, n_feat):
            peer = (feat + k) % n_feat
            copy = to_feat(peer, m_send.at[r, pl.ds(peer * own, own)], m_buf.at[r, feat], m_ssem.at[r, peer], m_rsem.at[r, feat])
            copy.start()
            sends.append(copy)
        for k in range(1, n_feat):
            peer = (feat + k) % n_feat
            to_feat(peer, m_buf.at[r, peer], m_buf.at[r, peer], m_ssem.at[r, peer], m_rsem.at[r, peer]).wait_recv()
        for copy in sends:
            copy.wait_send()

        squares = jnp.zeros((1, BLOCK), F32)
        dual_sum = jnp.zeros((1, BLOCK), F32)
        for k in range(own):
            value = m_buf[r, 0, k]
            for j in range(1, n_feat):
                value = value + m_buf[r, j, k]
            margins[k] = value
            goal, dual = wanted[first + k], duals[first + k]
            squares = squares + (value - goal) * (value - goal)
            dual_sum = dual_sum + (dual * goal - 0.5 * dual * dual)
        squares = jnp.sum(squares, axis=1, keepdims=True)
        dual_sum = jnp.sum(dual_sum, axis=1, keepdims=True)
        s_feat[feat, r] = jnp.where(lane == 0, squares, jnp.where(lane == 1, dual_sum, norm * (1.0 / n_samp)))
        return carry

    lax.fori_loop(0, ROUNDS, one_round, 0)

    sends = []
    for k in range(1, n_feat):
        peer = (feat + k) % n_feat
        copy = to_feat(peer, s_feat.at[feat], s_feat.at[feat], f_ssem.at[peer], f_rsem.at[feat])
        copy.start()
        sends.append(copy)

    w_out[...] = weights[...]
    restored = jnp.zeros((8, rows), F32)
    for b in range(blocks):
        restored = restored + nn(stacked(duals[b]), onehot[b * BLOCK:(b + 1) * BLOCK, :])
    duals_out[...] = unstacked(restored)

    for k in range(1, n_feat):
        peer = (feat + k) % n_feat
        to_feat(peer, s_feat.at[peer], s_feat.at[peer], f_ssem.at[peer], f_rsem.at[peer]).wait_recv()
    for copy in sends:
        copy.wait_send()
    total = s_feat[0]
    for k in range(1, n_feat):
        total = total + s_feat[k]
    s_samp[samp] = total
    sends = []
    for k in range(1, n_samp):
        peer = (samp + k) % n_samp
        copy = to_samp(peer, s_samp.at[samp], s_samp.at[samp], t_ssem.at[peer], t_rsem.at[samp])
        copy.start()
        sends.append(copy)
    for k in range(1, n_samp):
        peer = (samp + k) % n_samp
        to_samp(peer, s_samp.at[peer], s_samp.at[peer], t_ssem.at[peer], t_rsem.at[peer]).wait_recv()
    for copy in sends:
        copy.wait_send()
    total = s_samp[0]
    for k in range(1, n_samp):
        total = total + s_samp[k]
    penalty = 0.5 * ridge * total[:, :, 2:3]
    primal = total[:, :, 0:1] / (2.0 * sample_total) + penalty
    dual_value = total[:, :, 1:2] / sample_total - penalty
    obj_out[...] = jnp.where(lane[None] == 0, primal, dual_value)


def on_device(n_samp, n_feat, inputs, frequencies, phases, targets, block_order):
    rows = inputs.shape[0]
    width = frequencies.shape[1]
    blocks = rows // BLOCK
    own = blocks // n_feat
    dma = pltpu.SemaphoreType.DMA
    vmem = pl.BlockSpec(memory_space=pltpu.VMEM)
    weights, duals, objectives = pl.pallas_call(
        functools.partial(kernel, n_samp, n_feat),
        name="cocoa",
        out_shape=(
            jax.ShapeDtypeStruct((1, width), F32),
            jax.ShapeDtypeStruct((1, rows), F32),
            jax.ShapeDtypeStruct((ROUNDS, 1, LANES), F32),
        ),
        in_specs=[vmem] * 5,
        out_specs=(vmem, vmem, vmem),
        scratch_shapes=[
            pltpu.VMEM((rows, width), BF16),
            pltpu.VMEM((rows, rows), BF16),
            pltpu.VMEM((blocks, 1, BLOCK), F32),
            pltpu.VMEM((blocks, 1, BLOCK), F32),
            pltpu.VMEM((own, 1, BLOCK), F32),
            pltpu.VMEM((1, width), F32),
            pltpu.VMEM((8, width), F32),
            pltpu.VMEM((rows, LANES), F32),
            pltpu.VMEM((rows, LANES), F32),
            pltpu.VMEM((blocks, BLOCK, BLOCK), F32),
            pltpu.VMEM((n_feat, own, BLOCK, BLOCK), F32),
            pltpu.VMEM((own, BLOCK, BLOCK), F32),
            pltpu.VMEM((ROUNDS, blocks, 1, BLOCK), F32),
            pltpu.VMEM((ROUNDS, n_samp, 1, width), F32),
            pltpu.VMEM((ROUNDS, blocks, 1, BLOCK), F32),
            pltpu.VMEM((ROUNDS, n_feat, own, 1, BLOCK), F32),
            pltpu.VMEM((n_feat, ROUNDS, 1, LANES), F32),
            pltpu.VMEM((n_samp, ROUNDS, 1, LANES), F32),
            dma((n_feat, own)), dma((n_feat, own)),
            dma((ROUNDS, n_feat)), dma((ROUNDS, n_feat)),
            dma((ROUNDS, n_samp)), dma((ROUNDS, n_samp)),
            dma((ROUNDS, n_feat)), dma((ROUNDS, n_feat)),
            dma((n_feat,)), dma((n_feat,)),
            dma((n_samp,)), dma((n_samp,)),
        ],
        compiler_params=pltpu.CompilerParams(
            collective_id=0, has_side_effects=True, vmem_limit_bytes=60 * 2**20),
    )(inputs, frequencies, phases.reshape(1, width), targets.reshape(1, rows), block_order.reshape(rows, 1))
    return weights.reshape(width), duals.reshape(rows), objectives[:, 0, :2]


def solution(mesh):
    return jax.shard_map(
        functools.partial(on_device, mesh.shape["samp"], mesh.shape["feat"]),
        mesh=mesh,
        in_specs=(P("samp", None), P(None, "feat"), P("feat"), P("samp"), P("samp")),
        out_specs=(P("feat"), P("samp"), P()),
        check_vma=False,
    )
```

time: 619 us -> 146 us (0.24); the launches traced: 610 us -> 146 us
  matrix products: 215 us -> 0 us
  blocking collectives: 204 us -> 0 us
  Pallas kernels: 0 us -> 140 us
  other arithmetic: 119 us -> 0 us
  local copies, waits for them, and re-layouts: 33 us -> 6 us
  waiting for transfers between devices: 22.1 us -> 0 us
  between operations: 17.4 us -> 0.66 us
    dot_general x10 -> x0, matrix products: 207 us -> none  [the longest x1 120 us: on_device(): angles = jnp.dot(picked, frequencies, preferred_element_type=jnp.float32)]
    psum x9 -> x0, blocking collectives: 183 us -> none  [the longest x4 136 us: on_device(): weights = weights + lax.psum(step_term, 'samp')]
    pallas_call x0 -> x1, Pallas kernels: none -> 140 us  [on_device(): pl.pallas_call(functools.partial(kernel, n_samp, n_feat), name='cocoa', o...]
    another operation x28 -> x0, other arithmetic: 112 us -> none  [the longest x9 67.3 us: on_device(): factors = jnp.linalg.cholesky(gram_sums + jnp.eye(BLOCK, dtype=jnp.float32))]
    reduce_scatter x1 -> x0, waiting for transfers between devices: 22.1 us -> none  [on_device(): lax.psum_scatter(gram_sums, 'feat', scatter_dimension=0, tiled=True)]
    all_gather x4 -> x0, blocking collectives: 20.8 us -> none  [on_device(): lax.all_gather(own_update, 'feat', axis=0, tiled=True).reshape(row_count)]
    gather x2 -> x0, local copies, waits for them, and re-layouts: 18 us -> none  [the longest x1 11.8 us: on_device(): wanted = targets[block_order]]
    scatter x1 -> x0, local copies, waits for them, and re-layouts: 8.61 us -> none  [on_device(): restored = jnp.zeros_like(duals).at[block_order].set(duals)]
  transfers between devices with their start and end apart: 1 -> 0, of which waited for: 1 -> 0; matrix products, arithmetic and copies ran while one was open for 2% -> 0% of each run, Pallas kernels for 0% -> 0%
where the time goes in v1:
time: 146 us
  Pallas kernels  140 us (96%)
  local copies, waits for them, and re-layouts  6 us (4%)
    pallas_call x1, Pallas kernels, on_device(): pl.pallas_call(functools.partial(kernel, n_samp, n_feat), name='cocoa', o...  140 us
    unnamed x9, local copies, waits for them, and re-layouts  3.33 us

profile of v1, /device:TPU:0, one launch (start us, length us, event | category | flops | bytes accessed | tf_op | source)
XLA Modules:
  0.0 146.2 jit_solution(2249086234318288741)
XLA Ops:
  0.6 0.0 copy-start.1
  0.6 2.0 %copy.10.inputs = bf16[2048,96]{1,0:T(8,128)(2,1)} copy(bf16[2048,96]{0,1:T(8,128)(2,1)} %param.5) | data formatting | bytes 786432 | tf_op args[0]
  2.7 0.0 copy-done.1
  2.7 1.3 copy.11.order
  4.0 139.5 %cocoa.1 = (f32[1,4096]{1,0:T(1,128)}, f32[1,2048]{1,0:T(1,128)}, f32[4,1,128]{2,1,0:T(1,128)}) custom-call(bf16[2048,96]{1,0:T(8,128)(2,1)} %copy.10.inputs, bf16[96,4096]{1,0:T(8,128)(2,1)} %freqs.1, f32[1,4096]{1,0:T(1,128)} %bitcast.7, f32[1,2048]{1,0:T(1,128)} %bitcast.10, s32[2048,1]{1,0:T(8,128)} %copy.11.order), custom_call_target="tpu_custom_call" | custom-call | tf_op jit(solution)/shard_map/cocoa/pallas_call | solution.py:341
  143.5 0.0 copy-start
  143.6 1.3 copy.12
  144.9 0.0 copy-done
  144.9 0.0 copy-start.2
  144.9 0.6 copy.15
  145.5 0.1 copy-done.2
  145.6 0.6 copy.16
Async XLA Ops:
  0.6 2.0 %copy-start.1 = (s32[2048]{0:T(1024)S(1)}, s32[2048]{0:T(1024)}, u32[]{:S(2)}) copy-start(s32[2048]{0:T(1024)} %param.9) | copy-start | bytes 24580
  143.5 1.3 copy-start
  144.9 0.7 copy-start.2

commit v2 on v1

--- a/solution.py
+++ b/solution.py
@@ -14,6 +14,7 @@
 ROUNDS = 4
 LANES = 128
 CHUNK = 512
+PARTS = 2
 MESH = pl.DeviceIdType.MESH
 F32 = jnp.float32
 BF16 = jnp.bfloat16
@@ -71,7 +72,7 @@
 
 
 def kernel(n_samp, n_feat, inputs, freqs, phases, targets, order, w_out, duals_out, obj_out,
-           phi, onehot, wanted, duals, margins, weights, w_wide, d_col, y, gram, gram_in, inverse,
+           phi, onehot, wanted, duals, margins, weights, w_wide, y, gram, gram_in, inverse,
            d_buf, w_buf, m_send, m_buf, s_feat, s_samp,
            g_ssem, g_rsem, d_ssem, d_rsem, w_ssem, w_rsem, m_ssem, m_rsem, f_ssem, f_rsem, t_ssem, t_rsem):
     samp, feat = lax.axis_index("samp"), lax.axis_index("feat")
@@ -115,11 +116,16 @@
     def make_block(i, carry):
         block = owner_of(i // own) * own + i % own
         at = pl.ds(pl.multiple_of(block * BLOCK, BLOCK), BLOCK)
-        position = lax.broadcasted_iota(jnp.int32, (BLOCK, rows), 1)
-        hot = jnp.where(order[at, :] == position, 1.0, 0.0).astype(BF16)
+        position = lax.broadcasted_iota(jnp.int32, (LANES, rows), 1)
+        strips = []
+        for h in range(0, BLOCK, LANES):
+            place = order[:, pl.ds(pl.multiple_of(block * BLOCK + h, LANES), LANES)].astype(F32)
+            column = jnp.broadcast_to(place, (LANES, LANES)).T.astype(jnp.int32)[:, 0:1]
+            strips.append(jnp.where(column == position, 1.0, 0.0).astype(BF16))
+        hot = jnp.concatenate(strips, axis=0)
         onehot[at, :] = hot
         wanted[block] = unstacked(nt(target_rows, hot))
-        picked = nn(hot, inputs[...]).astype(BF16)
+        picked = nt(hot, inputs[...]).astype(BF16)
         total = None
         for c in range(0, width, CHUNK):
             turns = nn(picked, freqs[:, c:c + CHUNK]) + phases[:, c:c + CHUNK]
@@ -184,7 +190,8 @@
     weights[...] = jnp.zeros_like(weights)
     lane = lax.broadcasted_iota(jnp.int32, (1, LANES), 1)
     ones = jnp.ones((8, LANES), BF16)
-    tiles = width // LANES
+    piece = width // PARTS
+    step = min(CHUNK, piece)
 
     def one_round(r, carry):
         mine = pl.ds(first, own)
@@ -208,56 +215,57 @@
         for b in range(blocks):
             delta = d_buf[r, b]
             duals[b] = duals[b] + delta
-            rounded = delta.astype(BF16).astype(F32)
-            for h in range(0, BLOCK, LANES):
-                tile = jnp.broadcast_to(rounded[:, h:h + LANES], (LANES, LANES))
-                d_col[pl.ds(b * BLOCK + h, LANES), :] = tile.T
-
-        def down(g, sums):
-            at = pl.ds(pl.multiple_of(g * 16, 16), 16)
-            column = d_col[at, :]
-            result = []
-            for c in range(tiles):
-                term = phi[at, c * LANES:(c + 1) * LANES].astype(F32) * column
-                result.append(sums[c] + (term[0:8] + term[8:16]))
-            return tuple(result)
-
-        sums = lax.fori_loop(0, rows // 16, down, tuple(jnp.zeros((8, LANES), F32) for _ in range(tiles)))
-        for c in range(tiles):
-            w_buf[r, samp, :, c * LANES:(c + 1) * LANES] = jnp.sum(sums[c], axis=0, keepdims=True) * step_scale
+
+        moves = jnp.concatenate([jnp.broadcast_to(d_buf[r, b], (8, BLOCK)) for b in range(blocks)], axis=1).astype(BF16)
         sends = []
-        for k in range(1, n_samp):
-            peer = (samp + k) % n_samp
-            copy = to_samp(peer, w_buf.at[r, samp], w_buf.at[r, samp], w_ssem.at[r, peer], w_rsem.at[r, samp])
-            copy.start()
-            sends.append(copy)
-        for k in range(1, n_samp):
-            peer = (samp + k) % n_samp
-            to_samp(peer, w_buf.at[r, peer], w_buf.at[r, peer], w_ssem.at[r, peer], w_rsem.at[r, peer]).wait_recv()
+        for h in range(PARTS):
+            def down(c, carry):
+                w_buf[r, h, samp, c] = nn(moves, phi[:, pl.ds(pl.multiple_of(h * piece + c * step, step), step)])[0:1] * step_scale
+                return carry
+
+            lax.fori_loop(0, piece // step, down, 0)
+            for k in range(1, n_samp):
+                peer = (samp + k) % n_samp
+                copy = to_samp(peer, w_buf.at[r, h, samp], w_buf.at[r, h, samp], w_ssem.at[r, h, peer], w_rsem.at[r, h, samp])
+                copy.start()
+                sends.append(copy)
+
+        norm = jnp.zeros((1, 1), F32)
+        for h in range(PARTS):
+            for k in range(1, n_samp):
+                peer = (samp + k) % n_samp
+                to_samp(peer, w_buf.at[r, h, peer], w_buf.at[r, h, peer], w_ssem.at[r, h, peer], w_rsem.at[r, h, peer]).wait_recv()
+            for c in range(piece // step):
+                low = h * piece + c * step
+                change = w_buf[r, h, 0, c]
+                for k in range(1, n_samp):
+                    change = change + w_buf[r, h, k, c]
+                updated = weights[:, low:low + step] + change
+                weights[:, low:low + step] = updated
+                norm = norm + jnp.sum(updated * updated, axis=1, keepdims=True)
+                w_wide[:, low:low + step] = jnp.broadcast_to(updated.astype(BF16).astype(F32), (8, step))
+            start, split, stop = h * piece, h * piece + piece // 2, (h + 1) * piece
+            rounded = w_wide[:, start:split].astype(BF16)
+
+            def across(b, carry):
+                at = pl.ds(pl.multiple_of(b * BLOCK, BLOCK), BLOCK)
+                part = nt(rounded, phi[at, start:split])
+                total = jnp.zeros((BLOCK // 8, 8, LANES), F32) if h == 0 else y[at, :].reshape(BLOCK // 8, 8, LANES)
+                for c in range(split, stop, LANES):
+                    term = phi[at, c:c + LANES].astype(F32).reshape(BLOCK // 8, 8, LANES)
+                    total = total + term * w_wide[:, c:c + LANES][None]
+                total = total.reshape(BLOCK, LANES)
+                if h < PARTS - 1:
+                    y[at, :] = total
+                else:
+                    high, middle, low = thirds(total)
+                    part = part + (nt(ones, high) + (nt(ones, middle) + nt(ones, low)))
+                m_send[r, b] = part[0:1] if h == 0 else m_send[r, b] + part[0:1]
+                return carry
+
+            lax.fori_loop(0, blocks, across, 0)
         for copy in sends:
             copy.wait_send()
-
-        change = w_buf[r, 0]
-        for k in range(1, n_samp):
-            change = change + w_buf[r, k]
-        updated = weights[...] + change
-        weights[...] = updated
-        norm = jnp.sum(updated * updated, axis=1, keepdims=True)
-        w_wide[...] = jnp.broadcast_to(updated.astype(BF16).astype(F32), (8, width))
-
-        def across(g, carry):
-            at = pl.ds(pl.multiple_of(g * 32, 32), 32)
-            total = jnp.zeros((4, 8, LANES), F32)
-            for c in range(tiles):
-                term = phi[at, c * LANES:(c + 1) * LANES].astype(F32).reshape(4, 8, LANES)
-                total = total + term * w_wide[:, c * LANES:(c + 1) * LANES][None]
-            y[at, :] = total.reshape(32, LANES)
-            return carry
-
-        lax.fori_loop(0, rows // 32, across, 0)
-        for b in range(blocks):
-            high, middle, low = thirds(y[b * BLOCK:(b + 1) * BLOCK, :])
-            m_send[r, b] = (nt(ones, high) + (nt(ones, middle) + nt(ones, low)))[0:1]
         for k in range(own):
             m_buf[r, feat, k] = m_send[r, first + k]
         sends = []
@@ -357,26 +365,25 @@
             pltpu.VMEM((1, width), F32),
             pltpu.VMEM((8, width), F32),
             pltpu.VMEM((rows, LANES), F32),
-            pltpu.VMEM((rows, LANES), F32),
             pltpu.VMEM((blocks, BLOCK, BLOCK), F32),
             pltpu.VMEM((n_feat, own, BLOCK, BLOCK), F32),
             pltpu.VMEM((own, BLOCK, BLOCK), F32),
             pltpu.VMEM((ROUNDS, blocks, 1, BLOCK), F32),
-            pltpu.VMEM((ROUNDS, n_samp, 1, width), F32),
+            pltpu.VMEM((ROUNDS, PARTS, n_samp, width // PARTS // min(CHUNK, width // PARTS), 1, min(CHUNK, width // PARTS)), F32),
             pltpu.VMEM((ROUNDS, blocks, 1, BLOCK), F32),
             pltpu.VMEM((ROUNDS, n_feat, own, 1, BLOCK), F32),
             pltpu.VMEM((n_feat, ROUNDS, 1, LANES), F32),
             pltpu.VMEM((n_samp, ROUNDS, 1, LANES), F32),
             dma((n_feat, own)), dma((n_feat, own)),
             dma((ROUNDS, n_feat)), dma((ROUNDS, n_feat)),
-            dma((ROUNDS, n_samp)), dma((ROUNDS, n_samp)),
+            dma((ROUNDS, PARTS, n_samp)), dma((ROUNDS, PARTS, n_samp)),
             dma((ROUNDS, n_feat)), dma((ROUNDS, n_feat)),
             dma((n_feat,)), dma((n_feat,)),
             dma((n_samp,)), dma((n_samp,)),
         ],
         compiler_params=pltpu.CompilerParams(
             collective_id=0, has_side_effects=True, vmem_limit_bytes=60 * 2**20),
-    )(inputs, frequencies, phases.reshape(1, width), targets.reshape(1, rows), block_order.reshape(rows, 1))
+    )(inputs.T, frequencies, phases.reshape(1, width), targets.reshape(1, rows), block_order.reshape(1, rows))
     return weights.reshape(width), duals.reshape(rows), objectives[:, 0, :2]
 
 

time: 146 us -> 133 us (0.911)
  Pallas kernels: 140 us -> 129 us
  local copies, waits for them, and re-layouts: 6 us -> 2.62 us
    pallas_call x1, Pallas kernels: 140 us -> 129 us  [on_device(): pl.pallas_call(functools.partial(kernel, n_samp, n_feat), name='cocoa', o...]
    unnamed x9 -> x6, local copies, waits for them, and re-layouts: 3.33 us -> 1.31 us
where the time goes in v2:
time: 133 us
  Pallas kernels  129 us (97%)
  local copies, waits for them, and re-layouts  2.62 us (2%)
    pallas_call x1, Pallas kernels, on_device(): pl.pallas_call(functools.partial(kernel, n_samp, n_feat), name='cocoa', o...  129 us

profile of v2, /device:TPU:0, one launch (start us, length us, event | category | flops | bytes accessed | tf_op | source)
XLA Modules:
  0.0 132.6 jit_solution(17718582785269340988)
XLA Ops:
  0.6 129.3 %cocoa.1 = (f32[1,4096]{1,0:T(1,128)}, f32[1,2048]{1,0:T(1,128)}, f32[4,1,128]{2,1,0:T(1,128)}) custom-call(bf16[96,2048]{1,0:T(8,128)(2,1)} %bitcast.8, bf16[96,4096]{1,0:T(8,128)(2,1)} %freqs.1, f32[1,4096]{1,0:T(1,128)} %bitcast.9, f32[1,2048]{1,0:T(1,128)} %bitcast.11, s32[1,2048]{1,0:T(1,128)} %bitcast.12), custom_call_target="tpu_custom_call" | custom-call | tf_op jit(solution)/shard_map/cocoa/pallas_call | solution.py:349
  129.9 0.0 copy-start
  129.9 1.3 copy.8
  131.3 0.0 copy-done
  131.3 0.0 copy-start.1
  131.3 0.6 copy.11
  131.9 0.1 copy-done.1
  132.0 0.6 copy.12
Async XLA Ops:
  129.9 1.3 copy-start
  131.3 0.7 copy-start.1
